TPU v7x, 256 devices: a whole 4x4x8 slice. The times are simulated.
256 devices in a mesh: head: 8 (over x_hi, y), inner: 2 (over x_lo), outer: 16 (over z, core).
Axes of the slice: x: 4 (x_hi: 2, x_lo: 2; x = x_hi * 2 + x_lo), y: 4, z: 8, core: 2. Of those that a mesh axis runs over, the one named last changes fastest.
Arguments:
- query_nope: bfloat16 [4096, 8192], P(('inner', 'outer'), 'head'), may hold values from -6 to 6
- query_rope: bfloat16 [4096, 4096], P(('inner', 'outer'), 'head'), may hold values from -256 to 256
- latent: bfloat16 [4096, 512], P(('inner', 'outer')), may hold values from -6 to 6
- key_rope: bfloat16 [4096, 64], P(('inner', 'outer')), may hold values from -4 to 4
- key_up: bfloat16 [512, 8192], P(None, 'head'), may hold values from -0.25 to 0.25
- value_up: bfloat16 [512, 8192], P(None, 'head'), may hold values from -0.25 to 0.25
- latent_out: bfloat16 [4096, 32768], P(('inner', 'outer'), 'head'), may hold values from -3 to 3
- out_grad: bfloat16 [4096, 8192], P(('inner', 'outer'), 'head'), may hold values from -6 to 6
- logsum: float32 [4096, 64], P(('inner', 'outer'), 'head'), may hold values from 0 to 5000
- block_order: int32 [64], replicated, may hold values from 0 to 63, as said below
Outputs:
- d_query_nope: bfloat16 [4096, 8192], P(('inner', 'outer'), 'head')
- d_query_rope: bfloat16 [4096, 4096], P(('inner', 'outer'), 'head')
- d_latent: bfloat16 [4096, 512], P(('inner', 'outer'))
- d_key_rope: bfloat16 [4096, 64], P(('inner', 'outer'))
- d_key_up: float32 [512, 8192], P(('inner', 'outer'), 'head')
- d_value_up: float32 [512, 8192], P(('inner', 'outer'), 'head')
Inputs may be any that keep to these rules, and one draw needn't show every extreme that they name: `block_order`: stored blocks 2 r and 2 r + 1 hold sequence blocks c and 63 - c for some c, in either order; every sequence block is held once.
All inputs are finite; a program needn't handle non-finite values.
Results may differ from a plain program's by a relative error of at most 0.0085.
The roundings to bfloat16 on the way count: a program that leaves them out, or rounds other values in their place, can miss the bound.
Values may be sent and summed in bfloat16 or wider, within the bound.
No kernel may reach another device: no remote copies, remote signals or barrier semaphores. Data moves between devices by JAX's collectives and lax.ppermute only.
A program may use at most 128 MiB of HBM per device.

v0:
```python
import functools
import jax
import jax.numpy as jnp
from jax import lax
from jax.sharding import PartitionSpec as P

LATENT = 512
ROPE_DIM = 64
NOPE_DIM = 128
VALUE_DIM = 128


def split_up(shard, dim, count):
    shape = shard.shape
    pieces = shard.reshape(*shape[:dim], count, shape[dim] // count, *shape[dim + 1 :])
    return jnp.moveaxis(pieces, dim, 0)


def sum_packed(arrays, axis, dims):
    count = lax.axis_size(axis)
    pieces = [split_up(a, dim, count) for a, dim in zip(arrays, dims)]
    lines = jnp.concatenate([b.reshape(count, -1) for b in pieces], axis=1)
    width = max(16, -(-lines.shape[1] // 1024) * 8)
    lines = jnp.pad(lines, ((0, 0), (0, width * 128 - lines.shape[1]))).reshape(-1, 128)
    ravelled, at, gathered = (lax.psum_scatter(lines, axis, tiled=True).reshape(-1), 0, [])
    for b in pieces:
        part = b[0]
        gathered.append(ravelled[at : at + part.size].reshape(part.shape))
        at += part.size
    return tuple(gathered)


def sent_to_all(shard, axis):
    copies = jnp.broadcast_to(shard, (lax.axis_size(axis), *shard.shape))
    return lax.all_to_all(copies, axis, split_axis=0, concat_axis=0, tiled=True)


def of_everyone(shard, axis):
    everything = sent_to_all(shard, axis)
    return jnp.sum(everything, axis=0)


def in_one(arrays, axis):
    ends = [0]
    for a in arrays:
        ends.append(ends[-1] + a.size)
    subtotal = of_everyone(jnp.concatenate([a.ravel() for a in arrays]), axis)
    return tuple((subtotal[b:e].reshape(a.shape) for a, b, e in zip(arrays, ends, ends[1:])))


def side_by_side(arrays, axis, dim, along):
    ends, at = ([], 0)
    for a in arrays[:-1]:
        at += a.shape[along]
        ends.append(at)
    both = jnp.concatenate(arrays, axis=along)
    return tuple(
        jnp.split(lax.psum_scatter(both, axis, scatter_dimension=dim, tiled=True), ends, axis=along)
    )


def key_positions(block_order, first_row, length, block_size):
    indices = first_row + lax.iota(jnp.int32, length)
    owners = indices // block_size
    lookup = lax.iota(jnp.int32, block_order.shape[0])
    picked = (owners[:, None] == lookup[None, :]).astype(jnp.int32)
    return jnp.sum(picked * block_order[None, :], axis=1) * block_size + indices % block_size


def contract_last(first_op, second_op):
    return lax.dot_general(
        first_op, second_op, (((1,), (1,)), ((), ())), preferred_element_type=jnp.float32
    )


def contract_first(first_op, second_op):
    return lax.dot_general(
        first_op, second_op, (((0,), (0,)), ((), ())), preferred_element_type=jnp.float32
    )


def scaled_scores(queries, lat_keys, rope_keys):
    factor = float(NOPE_DIM + ROPE_DIM) ** (-0.5)
    return (contract_last(lat_keys, queries[0]) + contract_last(rope_keys, queries[1])) * factor


def unchanged(current):
    return current


def grad_update(carried, queries, lat_keys, rope_keys, positions):
    factor = float(NOPE_DIM + ROPE_DIM) ** (-0.5)
    scores = scaled_scores(queries, lat_keys, rope_keys)
    visible = positions[:, None] <= queries[2][None, :]
    weights = jnp.where(
        visible, jnp.exp(jnp.where(visible, scores - queries[5][None, :], 0.0)), 0.0
    )
    dprobs = contract_last(lat_keys, queries[3])
    dscore = (weights * (dprobs - queries[4][None, :]) * factor).astype(jnp.bfloat16)
    rounded = weights.astype(jnp.bfloat16)
    return (
        carried[0] + contract_first(dscore, lat_keys),
        carried[1] + contract_first(dscore, rope_keys),
        carried[2]
        + jnp.dot(dscore, queries[0], preferred_element_type=jnp.float32)
        + jnp.dot(rounded, queries[3], preferred_element_type=jnp.float32),
        carried[3] + jnp.dot(dscore, queries[1], preferred_element_type=jnp.float32),
    )


def single_block(carried, queries, lat_keys, rope_keys, positions, offset, block_size):
    part_lat = lax.dynamic_slice_in_dim(lat_keys, offset, block_size, 0)
    part_rope = lax.dynamic_slice_in_dim(rope_keys, offset, block_size, 0)
    part_pos = lax.dynamic_slice_in_dim(positions, offset, block_size, 0)
    sum_lat = lax.dynamic_slice_in_dim(carried[2], offset, block_size, 0)
    sum_rope = lax.dynamic_slice_in_dim(carried[3], offset, block_size, 0)
    result = grad_update(
        (carried[0], carried[1], sum_lat, sum_rope), queries, part_lat, part_rope, part_pos
    )
    return (
        result[0],
        result[1],
        lax.dynamic_update_slice_in_dim(carried[2], result[2], offset, 0),
        lax.dynamic_update_slice_in_dim(carried[3], result[3], offset, 0),
    )


def shard_grads(query_pairs, query_grads, lat_keys, rope_keys, positions):
    block_size = lat_keys.shape[0] // 2
    key_lat = jnp.zeros(lat_keys.shape, jnp.float32)
    key_rope_acc = jnp.zeros(rope_keys.shape, jnp.float32)
    updated = []
    for target in range(2):
        queries = query_pairs[target]
        latest = queries[2][-1]
        first_seen = positions[0] <= latest
        second_seen = positions[block_size] <= latest
        branch_index = first_seen.astype(jnp.int32) + second_seen.astype(jnp.int32)
        offset = jnp.where(first_seen, 0, block_size).astype(jnp.int32)
        whole = functools.partial(
            grad_update,
            queries=queries,
            lat_keys=lat_keys,
            rope_keys=rope_keys,
            positions=positions,
        )
        single = functools.partial(
            single_block,
            queries=queries,
            lat_keys=lat_keys,
            rope_keys=rope_keys,
            positions=positions,
            offset=offset,
            block_size=block_size,
        )
        carried = lax.switch(
            branch_index,
            [unchanged, single, whole],
            (query_grads[target][0], query_grads[target][1], key_lat, key_rope_acc),
        )
        updated.append((carried[0], carried[1]))
        key_lat, key_rope_acc = (carried[2], carried[3])
    return (tuple(updated), (key_lat, key_rope_acc))


def local(
    query_nope,
    query_rope,
    latent,
    key_rope,
    key_up,
    value_up,
    latent_out,
    out_grad,
    logsum,
    block_order,
):
    tokens = query_nope.shape[0]
    head_count = query_nope.shape[1] // NOPE_DIM
    block_size = tokens // 2
    flat_rows = block_size * head_count
    nope_heads = query_nope.reshape(tokens, head_count, NOPE_DIM)
    rope_heads = query_rope.reshape(tokens, head_count, ROPE_DIM)
    saved = latent_out.reshape(tokens, head_count, LATENT)
    upstream = out_grad.reshape(tokens, head_count, VALUE_DIM)
    key_map = key_up.reshape(LATENT, head_count, NOPE_DIM)
    value_map = value_up.reshape(LATENT, head_count, VALUE_DIM)
    query_latent = jnp.einsum(
        "thn,lhn->thl", nope_heads, key_map, preferred_element_type=jnp.float32
    ).astype(jnp.bfloat16)
    grad_latent = jnp.einsum(
        "thv,lhv->thl", upstream, value_map, preferred_element_type=jnp.float32
    ).astype(jnp.bfloat16)
    row_delta = jnp.sum(grad_latent.astype(jnp.float32) * saved.astype(jnp.float32), axis=2)
    context_size = lax.axis_size(("inner", "outer"))
    my_index = lax.axis_index(("inner", "outer"))
    own_positions = key_positions(block_order, my_index * tokens, tokens, block_size)
    query_parts = []
    for target in range(2):
        offset = target * block_size
        positions = jnp.broadcast_to(
            own_positions[offset : offset + block_size, None], (block_size, head_count)
        ).reshape(flat_rows)
        lat_part = query_latent[offset : offset + block_size].reshape(flat_rows, LATENT)
        rope_part = rope_heads[offset : offset + block_size].reshape(flat_rows, ROPE_DIM)
        grad_part = grad_latent[offset : offset + block_size].reshape(flat_rows, LATENT)
        delta_part = row_delta[offset : offset + block_size].reshape(flat_rows)
        total_part = logsum[offset : offset + block_size].reshape(flat_rows)
        query_parts.append((lat_part, rope_part, positions, grad_part, delta_part, total_part))
    backward_pairs = tuple(query_parts)
    zero_grads = tuple(
        (
            (
                jnp.zeros((flat_rows, LATENT), jnp.float32),
                jnp.zeros((flat_rows, ROPE_DIM), jnp.float32),
            )
            for target in range(2)
        )
    )
    every_lat, every_rope = (
        lax.all_gather(latent, ("inner", "outer"), axis=0, tiled=True),
        lax.all_gather(key_rope, ("inner", "outer"), axis=0, tiled=True),
    )

    def visit_pair(query_grads, turn_index):
        lat_rows = []
        rope_rows = []
        for member in range(2):
            shard_index = 2 * turn_index + member
            lat_keys = lax.dynamic_slice_in_dim(every_lat, shard_index * tokens, tokens, 0)
            rope_keys = lax.dynamic_slice_in_dim(every_rope, shard_index * tokens, tokens, 0)
            positions = key_positions(block_order, shard_index * tokens, tokens, block_size)
            query_grads, contribution = shard_grads(
                backward_pairs, query_grads, lat_keys, rope_keys, positions
            )
            lat_rows.append(contribution[0])
            rope_rows.append(contribution[1])
        return (query_grads, (jnp.stack(lat_rows), jnp.stack(rope_rows)))

    query_grads, stacked = lax.scan(visit_pair, zero_grads, lax.iota(jnp.int32, context_size // 2))
    all_lat = stacked[0].reshape(context_size * tokens, LATENT)
    all_rope = stacked[1].reshape(context_size * tokens, ROPE_DIM)
    own_sums = sum_packed((all_lat, all_rope), ("inner", "outer"), (0, 0))
    summed = in_one((own_sums[0], own_sums[1]), "head")
    grad_query = jnp.concatenate([query_grads[0][0], query_grads[1][0]], axis=0)
    grad_query = grad_query.reshape(tokens, head_count, LATENT).astype(jnp.bfloat16)
    grad_rope = jnp.concatenate([query_grads[0][1], query_grads[1][1]], axis=0)
    d_query_rope = grad_rope.reshape(tokens, head_count * ROPE_DIM).astype(jnp.bfloat16)
    d_query_nope = jnp.einsum(
        "thl,lhn->thn", grad_query, key_map, preferred_element_type=jnp.float32
    )
    d_query_nope = d_query_nope.reshape(tokens, head_count * NOPE_DIM).astype(jnp.bfloat16)
    key_weight = jnp.einsum(
        "thl,thn->lhn", grad_query, nope_heads, preferred_element_type=jnp.float32
    )
    value_weight = jnp.einsum("thl,thv->lhv", saved, upstream, preferred_element_type=jnp.float32)
    weight_parts = side_by_side(
        (
            key_weight.reshape(LATENT, head_count * NOPE_DIM),
            value_weight.reshape(LATENT, head_count * VALUE_DIM),
        ),
        ("inner", "outer"),
        0,
        1,
    )
    return (
        d_query_nope,
        d_query_rope,
        summed[0].astype(jnp.bfloat16),
        summed[1].astype(jnp.bfloat16),
        weight_parts[0],
        weight_parts[1],
    )


def solution(mesh):
    placed = (
        P(("inner", "outer"), "head"),
        P(("inner", "outer"), "head"),
        P(("inner", "outer"), None),
        P(("inner", "outer"), None),
        P(None, "head"),
        P(None, "head"),
        P(("inner", "outer"), "head"),
        P(("inner", "outer"), "head"),
        P(("inner", "outer"), "head"),
        P(),
    )
    return jax.shard_map(
        local,
        mesh=mesh,
        in_specs=placed,
        out_specs=(
            P(("inner", "outer"), "head"),
            P(("inner", "outer"), "head"),
            P(("inner", "outer"), None),
            P(("inner", "outer"), None),
            P(("inner", "outer"), "head"),
            P(("inner", "outer"), "head"),
        ),
        check_vma=False,
    )
```

profile of v0, /device:TPU:4, one launch (start us, length us, event | category | flops | bytes accessed | tf_op | source)
XLA Modules:
  0.0 1753.0 jit_solution(2727139085759418729)
XLA Ops:
  26.4 42.7 %all_gather.7 = bf16[4096,64]{1,0:T(8,128)(2,1)} all-gather(bf16[128,64]{1,0:T(8,128)(2,1)S(1)} %copy.107), channel_id=1, replica_groups=mesh['head'=8,'inner'=2,'outer'=16] {'inner','outer'}, dimensions={0}, use_global_device_ids=true | all-gather | bytes 540672 | tf_op jit(solution)/shard_map/all_gather | solution.py:222
  82.8 977.8 %while.24 = (s32[]{:T(128)}, f32[512,512]{1,0:T(8,128)S(1)}, f32[512,64]{0,1:T(8,128)}, f32[512,512]{1,0:T(8,128)}, f32[512,64]{0,1:T(8,128)}, /*index=5*/f32[16...) while((s32[]{:T(128)}, f32[512,512]{1,0:T(8,128)S(1)}, ...), condition=%wide.region_17.18_spmd.clone, body=%wide.region_2.17_spmd.clone.sunk | while | flops 1447517440 | bytes 55401404 | solution.py:240
  109.5 16.2 conditional.14
  129.4 14.1 conditional.13
  146.0 16.0 conditional.15
  195.7 10.3 conditional.13
  223.7 14.0 conditional.12
  242.2 16.2 conditional.14
  308.6 10.3 conditional.13
  336.6 14.0 conditional.12
  355.0 16.1 conditional.14
  374.9 14.0 conditional.13
  391.4 15.9 conditional.15
  441.0 10.3 conditional.13
  562.1 14.0 conditional.12
  580.5 16.1 conditional.14
  628.3 14.0 conditional.12
  646.8 16.1 conditional.14
  666.6 14.0 conditional.13
  683.1 15.9 conditional.15
  714.2 14.0 conditional.12
  732.6 16.1 conditional.14
  780.4 14.0 conditional.12
  798.9 16.2 conditional.14
  865.4 10.3 conditional.13
  911.9 14.1 conditional.13
  928.4 16.0 conditional.15
  959.7 14.0 conditional.12
  978.1 16.1 conditional.14
  1060.6 11.6 copy.143
  1105.4 511.1 %reduce-scatter.3.cloned.1.call-done = f32[576,128]{1,0:T(8,128)} async-done(((f32[18432,128]{1,0:T(8,128)}), f32[576,128]{1,0:T(8,128)}) %reduce-scatter.3.cloned.1.call-update) | async-done | bytes 294928 | tf_op jit(solution)/shard_map/reduce_scatter | solution.py:25
  1631.6 108.3 %reduce-scatter.5.cloned.1.call-done = f32[16,2048]{1,0:T(8,128)} async-done(((f32[512,2048]{1,0:T(8,128)}), f32[16,2048]{1,0:T(8,128)}) %reduce-scatter.5.cloned.1.call-update) | async-done | bytes 131088 | tf_op jit(solution)/shard_map/reduce_scatter | solution.py:58
  (1246 shorter events, 1057.2 us)
Async XLA Ops:
  7.2 10.8 copy-start
  7.2 72.5 %all-gather.2.cloned.1.call-start = ((), (), s32[]{:S(2)}) async-start(), calls=%async_computation.3 | async-start | bytes 4325376 | tf_op jit(solution)/shard_map/all_gather | solution.py:221
  7.9 1608.6 %reduce-scatter.3.cloned.1.call-start = ((), (), s32[]{:S(2)}) async-start(), calls=%async_computation.4 | async-start | bytes 9732096 | tf_op jit(solution)/shard_map/reduce_scatter | solution.py:25
  9.6 11.2 copy-start.36
  11.0 13.2 copy-start.45
  16.6 54.2 %copy-start.38 = (bf16[512,1024]{0,1:T(8,128)(2,1)}, bf16[512,1024]{0,1:T(8,128)(2,1)S(1)}, u32[]{:S(2)}) copy-start(bf16[512,1024]{0,1:T(8,128)(2,1)S(1)} %copy.139) | copy-start | bytes 3145732
  18.0 52.9 %copy-start.41 = (bf16[128,1024]{0,1:T(8,128)(2,1)}, bf16[128,1024]{0,1:T(8,128)(2,1)S(1)}, u32[]{:S(2)}) copy-start(bf16[128,1024]{0,1:T(8,128)(2,1)S(1)} %copy.140) | copy-start | bytes 786436
  129.4 16.6 copy-start.7
  195.7 12.8 copy-start.7
  249.0 6.9 copy-start.8
  262.1 12.8 copy-start.7
  308.6 12.8 copy-start.7
  374.9 16.5 copy-start.7
  441.0 12.8 copy-start.7
  487.5 12.8 copy-start.7
  534.1 12.8 copy-start.7
  600.3 12.8 copy-start.7
  666.6 16.5 copy-start.7
  739.4 6.9 copy-start.8
  752.4 12.8 copy-start.7
  818.9 12.8 copy-start.7
  865.4 12.8 copy-start.7
  911.9 16.6 copy-start.7
  997.9 12.8 copy-start.7
  1044.5 12.8 copy-start.7
  1091.7 648.3 %reduce-scatter.5.cloned.1.call-start = ((), (), s32[]{:S(2)}) async-start(), calls=%async_computation.5 | async-start | bytes 4325376 | tf_op jit(solution)/shard_map/reduce_scatter | solution.py:58
  1097.9 7.5 copy-start.40
  1617.3 10.6 copy-start.18
  1618.3 9.6 copy-start.27
  1618.3 10.6 copy-start.39
  1621.0 120.5 %all-to-all-start = ((f32[8,1,73728]{2,1,0:T(1,128)}), f32[8,1,73728]{2,1,0:T(1,128)}, u32[]{:S(2)}, u32[]{:S(2)}) async-start(f32[8,1,73728]{2,1,0:T(1,128)} %broadcast_in_dim.92), calls=%async_computation.1 | async-start | bytes 4718592 | tf_op jit(solution)/shard_map/all_to_all | solution.py:35
  1627.8 118.6 %copy-start.1 = (bf16[512,1024]{1,0:T(8,128)(2,1)S(1)}, bf16[512,1024]{1,0:T(8,128)(2,1)}, u32[]{:S(2)}) copy-start(bf16[512,1024]{1,0:T(8,128)(2,1)} %param.29) | copy-start | bytes 3145732
  (143 other events, 508.1 us)
Sparse Core Ops, SparseCore 0:
  9.9 69.7 all-gather.1
  1091.8 524.6 reduce-scatter.2
  1619.0 120.8 reduce-scatter.4
where the time goes:
time: 1790 us; the launch traced here: 1750 us
  waiting for transfers between devices  628 us (35%)
  matrix products  393 us (22%)
  local copies, waits for them, and re-layouts  383 us (21%)
  loops' own time  184 us (10%)
  other arithmetic  102 us (6%)
  blocking collectives  42.7 us (2%)
    reduce_scatter x1, waiting for transfers between devices, sum_packed(): lax.psum_scatter(lines, axis, tiled=True).reshape(-1)  511 us
    dot_general x132, matrix products, contract_last(): lax.dot_general(first_op, second_op, (((1,), (1,)), ((), ())), preferred_...  197 us
    another operation x1, loops' own time, local(): lax.scan(visit_pair, zero_grads, lax.iota(jnp.int32, context_size // 2))  179 us
    reduce_scatter x1, waiting for transfers between devices, side_by_side(): lax.psum_scatter(both, axis, scatter_dimension=dim, tiled=True)  108 us
    dot_general x44, matrix products, grad_update(): jnp.dot(rounded, queries[3], preferred_element_type=jnp.float32)  79.8 us
    dynamic_update_slice x32, other arithmetic, local(): lax.scan(visit_pair, zero_grads, lax.iota(jnp.int32, context_size // 2))  52.3 us
    dot_general x88, matrix products, contract_first(): lax.dot_general(first_op, second_op, (((0,), (0,)), ((), ())), preferred_...  50.4 us
    all_gather x1, blocking collectives, local(): lax.all_gather(key_rope, ('inner', 'outer'), axis=0, tiled=True)  42.7 us
  transfers between devices with their start and end apart: 4, of which 3 were waited for; matrix products, arithmetic and copies ran while one was open for 2% of the time, Pallas kernels for 0%

commit v1 on v0

--- a/solution.py
+++ b/solution.py
@@ -219,7 +219,12 @@
     )
     every_lat, every_rope = (
         lax.all_gather(latent, ("inner", "outer"), axis=0, tiled=True),
-        lax.all_gather(key_rope, ("inner", "outer"), axis=0, tiled=True),
+        jnp.concatenate(
+            lax.all_to_all(
+                jnp.stack([key_rope] * lax.axis_size(("inner", "outer"))), ("inner", "outer"), 0, 0
+            ),
+            axis=0,
+        ),
     )
 
     def visit_pair(query_grads, turn_index):

time: 1790 us -> 1800 us (level)
  blocking collectives: 42.7 us -> 0 us
  waiting for transfers between devices: 628 us -> 661 us
    all_gather x1 -> x0, blocking collectives: 42.7 us -> none  [local(): lax.all_gather(key_rope, ('inner', 'outer'), axis=0, tiled=True)]
    all_gather x1, waiting for transfers between devices: 7.51 us -> 39.7 us  [local(): lax.all_gather(latent, ('inner', 'outer'), axis=0, tiled=True)]
  transfers between devices with their start and end apart: 4 -> 5, of which waited for: 3 -> 4; matrix products, arithmetic and copies ran while one was open for 2% -> 3% of each run, Pallas kernels for 0% -> 0%
where the time goes in v1:
time: 1800 us; the launch traced here: 1760 us
  waiting for transfers between devices  661 us (37%)
  matrix products  394 us (22%)
  local copies, waits for them, and re-layouts  389 us (22%)
  loops' own time  186 us (10%)
  other arithmetic  101 us (6%)
    reduce_scatter x1, waiting for transfers between devices, sum_packed(): lax.psum_scatter(lines, axis, tiled=True).reshape(-1)  510 us
    dot_general x132, matrix products, contract_last(): lax.dot_general(first_op, second_op, (((1,), (1,)), ((), ())), preferred_...  197 us
    another operation x1, loops' own time, local(): lax.scan(visit_pair, zero_grads, lax.iota(jnp.int32, context_size // 2))  182 us
    reduce_scatter x1, waiting for transfers between devices, side_by_side(): lax.psum_scatter(both, axis, scatter_dimension=dim, tiled=True)  110 us
    dot_general x44, matrix products, grad_update(): jnp.dot(rounded, queries[3], preferred_element_type=jnp.float32)  80.2 us
    dynamic_update_slice x32, other arithmetic, local(): lax.scan(visit_pair, zero_grads, lax.iota(jnp.int32, context_size // 2))  52.5 us
    dot_general x88, matrix products, contract_first(): lax.dot_general(first_op, second_op, (((0,), (0,)), ((), ())), preferred_...  50.4 us
    slice x32, local copies, waits for them, and re-layouts, shard_grads(): latest = queries[2][-1]  41.1 us
  transfers between devices with their start and end apart: 5, of which 4 were waited for; matrix products, arithmetic and copies ran while one was open for 3% of the time, Pallas kernels for 0%

profile of v1, /device:TPU:4, one launch (start us, length us, event | category | flops | bytes accessed | tf_op | source)
XLA Modules:
  0.0 1763.4 jit_solution(15762667196714580868)
XLA Ops:
  42.9 39.7 %all-gather.2.cloned.1.call-done = bf16[4096,512]{1,0:T(8,128)(2,1)} async-done(((bf16[128,512]{1,0:T(8,128)(2,1)}), bf16[4096,512]{1,0:T(8,128)(2,1)}) %all-gather.2.cloned.1.call-update) | async-done | bytes 4194320 | tf_op jit(solution)/shard_map/all_gather | solution.py:221
  85.7 984.7 %while.24 = (s32[]{:T(128)}, f32[512,512]{1,0:T(8,128)S(1)}, f32[512,64]{0,1:T(8,128)}, f32[512,512]{1,0:T(8,128)}, f32[512,64]{0,1:T(8,128)}, /*index=5*/f32[16...) while((s32[]{:T(128)}, f32[512,512]{1,0:T(8,128)S(1)}, ...), condition=%wide.region_17.18_spmd.clone, body=%wide.region_2.17_spmd.clone.sunk | while | flops 1447517440 | bytes 55401404 | solution.py:245
  97.5 10.4 conditional.12
  112.3 16.3 conditional.14
  132.5 14.2 conditional.13
  149.3 16.1 conditional.15
  180.5 10.4 conditional.12
  227.4 14.1 conditional.12
  245.9 16.3 conditional.14
  341.1 14.0 conditional.12
  359.6 16.2 conditional.14
  379.7 14.1 conditional.13
  396.5 16.0 conditional.15
  427.5 10.4 conditional.12
  474.4 10.4 conditional.12
  568.2 14.0 conditional.12
  586.6 16.2 conditional.14
  634.9 14.0 conditional.12
  653.4 16.2 conditional.14
  673.5 14.1 conditional.13
  690.2 16.0 conditional.15
  721.3 14.0 conditional.12
  739.8 16.2 conditional.14
  788.0 14.1 conditional.12
  806.6 16.3 conditional.14
  920.5 14.2 conditional.13
  937.3 16.1 conditional.15
  968.5 14.0 conditional.12
  987.0 16.2 conditional.14
  1070.3 11.6 copy.174
  1116.8 510.1 %reduce-scatter.3.cloned.1.call-done = f32[576,128]{1,0:T(8,128)} async-done(((f32[18432,128]{1,0:T(8,128)}), f32[576,128]{1,0:T(8,128)}) %reduce-scatter.3.cloned.1.call-update) | async-done | bytes 294928 | tf_op jit(solution)/shard_map/reduce_scatter | solution.py:25
  1640.8 109.6 %reduce-scatter.5.cloned.1.call-done = f32[16,2048]{1,0:T(8,128)} async-done(((f32[512,2048]{1,0:T(8,128)}), f32[16,2048]{1,0:T(8,128)}) %reduce-scatter.5.cloned.1.call-update) | async-done | bytes 131088 | tf_op jit(solution)/shard_map/reduce_scatter | solution.py:58
  (1246 shorter events, 1068.1 us)
Async XLA Ops:
  7.2 22.2 %copy-start = (bf16[512,1024]{1,0:T(8,128)(2,1)S(1)}, bf16[512,1024]{1,0:T(8,128)(2,1)}, u32[]{:S(2)}) copy-start(bf16[512,1024]{1,0:T(8,128)(2,1)} %param.29) | copy-start | bytes 3145732
  7.2 15.1 copy-start.42
  7.2 75.4 %all-gather.2.cloned.1.call-start = ((), (), s32[]{:S(2)}) async-start(), calls=%async_computation.4 | async-start | bytes 4325376 | tf_op jit(solution)/shard_map/all_gather | solution.py:221
  9.6 31.0 %all-to-all-start = ((bf16[32,128,64]{1,2,0:T(8,128)(2,1)}), bf16[32,128,64]{1,2,0:T(8,128)(2,1)}, u32[]{:S(2)}, u32[]{:S(2)}) async-start(bf16[32,128,64]{1,2,0:T(8,128)(2,1)} %stack.101), calls=%async_computation | async-start | bytes 1048576 | tf_op jit(solution)/shard_map/all_to_all | solution.py:223
  19.2 1607.7 %reduce-scatter.3.cloned.1.call-start = ((), (), s32[]{:S(2)}) async-start(), calls=%async_computation.5 | async-start | bytes 9732096 | tf_op jit(solution)/shard_map/reduce_scatter | solution.py:25
  20.9 11.3 copy-start.36
  20.9 12.8 copy-start.43
  22.2 12.4 copy-start.44
  28.0 9.9 copy-start.38
  29.3 8.6 copy-start.40
  132.5 16.8 copy-start.7
  199.3 13.0 copy-start.7
  266.1 13.0 copy-start.7
  313.0 13.0 copy-start.7
  379.7 16.7 copy-start.7
  446.3 13.0 copy-start.7
  493.2 13.0 copy-start.7
  540.0 13.0 copy-start.7
  606.8 13.0 copy-start.7
  673.5 16.7 copy-start.7
  759.9 13.0 copy-start.7
  826.8 13.0 copy-start.7
  873.7 13.0 copy-start.7
  920.5 16.8 copy-start.7
  1007.1 13.0 copy-start.7
  1054.0 13.0 copy-start.7
  1101.5 648.9 %reduce-scatter.5.cloned.1.call-start = ((), (), s32[]{:S(2)}) async-start(), calls=%async_computation.6 | async-start | bytes 4325376 | tf_op jit(solution)/shard_map/reduce_scatter | solution.py:58
  1627.7 10.6 copy-start.18
  1628.7 9.6 copy-start.27
  1628.7 10.7 copy-start.39
  1631.4 120.5 %all-to-all-start.1 = ((f32[8,1,73728]{2,1,0:T(1,128)}), f32[8,1,73728]{2,1,0:T(1,128)}, u32[]{:S(2)}, u32[]{:S(2)}) async-start(f32[8,1,73728]{2,1,0:T(1,128)} %broadcast_in_dim.92), calls=%async_computation.2 | async-start | bytes 4718592 | tf_op jit(solution)/shard_map/all_to_all | solution.py:35
  1638.2 118.6 %copy-start.1 = (bf16[512,1024]{1,0:T(8,128)(2,1)S(1)}, bf16[512,1024]{1,0:T(8,128)(2,1)}, u32[]{:S(2)}) copy-start(bf16[512,1024]{1,0:T(8,128)(2,1)} %param.29) | copy-start | bytes 3145732
  (143 other events, 517.1 us)
Sparse Core Ops, SparseCore 0:
  9.9 72.6 all-gather.1
  1101.6 525.2 reduce-scatter.2
  1629.4 120.8 reduce-scatter.4
